TPU v7x, 768 devices: a whole 4x8x12 slice. The times are simulated.
768 devices in a mesh: section: 32 (over x_hi, y, core), tensor: 24 (over z, x_lo).
Axes of the slice: x: 4 (x_hi: 2, x_lo: 2; x = x_hi * 2 + x_lo), y: 8, z: 12, core: 2. Of those that a mesh axis runs over, the one named last changes fastest.
Arguments:
- section_inputs: bfloat16 [32, 3072, 1024], P('section', 'tensor'), may hold values from -6 to 6
- w_in: bfloat16 [32, 2304, 1024], P('section', 'tensor'), may hold values from -0.1875 to 0.1875
- in_bias: bfloat16 [32, 2304], P('section', 'tensor'), may hold values from -3 to 3
- w_out: bfloat16 [32, 2304, 1024], P('section', 'tensor'), may hold values from -0.125 to 0.125
- out_bias: float32 [32, 1024], P('section'), may hold values from -2 to 2
- norm_gain: float32 [32, 1024], P('section'), may hold values from 0.1 to 1.9
- norm_bias: float32 [32, 1024], P('section'), may hold values from -2 to 2
- patches: bfloat16 [8, 3072, 1024], P(None, 'tensor'), may hold values from -6 to 6
- plan: int32 [3], replicated, may hold values from 0 to 7, as said below
Outputs:
- received: bfloat16 [32, 4, 3072, 1024], P('section', None, 'tensor')
Inputs may be any that keep to these rules, and one draw needn't show every extreme that they name: `plan`: the first min(8, 3) entries are all different.
All inputs are finite; a program needn't handle non-finite values.
Results may differ from a plain program's by a relative error of at most 0.0065.
Values may be sent and summed in bfloat16 or wider, within the bound.
A program may use at most 64 MiB of HBM per device.

v0:
```python
import jax
import jax.numpy as jnp
from jax import lax
from jax.sharding import PartitionSpec as P

TICKS = 4


norm_floor = 0.1
gelu_slope = 1.702


def side_by_side(arrays, axis, dim, along):
    columns = [a.reshape(*a.shape[:along], -1) for a in arrays]
    both = jnp.concatenate(columns, axis=along)
    out, at, outs = (lax.all_gather(both, axis, axis=dim, tiled=True), 0, [])
    for a, column in zip(arrays, columns):
        piece = out[..., at : at + column.shape[along]]
        outs.append(piece.reshape(*piece.shape[:along], *a.shape[along:]))
        at += column.shape[along]
    return tuple(outs)


def passed_along(value, axis, steps):
    count = lax.axis_size(axis)
    pairs = [(source, (source + steps) % count) for source in range(count)]
    return lax.ppermute(value, axis, pairs)


def normalize(current, gain_row, shift_row):
    widened = current.astype(jnp.float32)
    average = jnp.mean(widened, axis=-1, keepdims=True)
    centered = widened - average
    variance = jnp.mean(centered * centered, axis=-1, keepdims=True)
    normed = (centered * lax.rsqrt(variance + norm_floor) * gain_row + shift_row).astype(
        jnp.bfloat16
    )
    return (normed, widened)


def activate(preact):
    return preact * jax.nn.sigmoid(gelu_slope * preact)


def hidden_units(normed, rows_in, rows_bias):
    preact = lax.dot_general(
        normed, rows_in, (((1,), (1,)), ((), ())), preferred_element_type=jnp.float32
    )
    return activate(preact + rows_bias.astype(jnp.float32)).astype(jnp.bfloat16)


def apply_block(current, gain_row, shift_row, full_in, full_bias, full_out, bias_row):
    normed, widened = normalize(current, gain_row, shift_row)
    hidden = hidden_units(normed, full_in, full_bias)
    return (
        widened + jnp.dot(hidden, full_out, preferred_element_type=jnp.float32) + bias_row
    ).astype(jnp.bfloat16)


def shards(section_inputs, w_in, in_bias, w_out, out_bias, norm_gain, norm_bias, patches, plan):
    current = section_inputs[0]
    gain_row = norm_gain[0]
    shift_row = norm_bias[0]
    bias_row = out_bias[0]
    section_index = lax.axis_index("section")
    full_in, full_bias, full_out = side_by_side((w_in[0], in_bias[0], w_out[0]), "tensor", 0, 1)
    produced = apply_block(current, gain_row, shift_row, full_in, full_bias, full_out, bias_row)
    records = []
    for tick_index in range(TICKS):
        if tick_index > 0:
            produced = apply_block(
                current, gain_row, shift_row, full_in, full_bias, full_out, bias_row
            )
        arrived = passed_along(produced, "section", 1)
        records.append(arrived)
        if tick_index + 1 < TICKS:
            selected = lax.dynamic_index_in_dim(patches, plan[tick_index], 0, keepdims=False)
            current = jnp.where(section_index == 0, selected, arrived)
    return jnp.stack(records, axis=0)[None]


def solution(mesh):
    placed = (
        P("section", "tensor", None),
        P("section", "tensor", None),
        P("section", "tensor"),
        P("section", "tensor", None),
        P("section", None),
        P("section", None),
        P("section", None),
        P(None, "tensor", None),
        P(),
    )
    return jax.shard_map(
        shards,
        mesh=mesh,
        in_specs=placed,
        out_specs=P("section", None, "tensor", None),
        check_vma=False,
    )
```

profile of v0, /device:TPU:66, one launch (start us, length us, event | category | flops | bytes accessed | tf_op | source)
XLA Modules:
  0.0 329.3 jit_solution(10678083976727927273)
XLA Ops:
  6.5 0.0 copy-start
  6.5 0.0 all-gather.2.cloned.1.call-start
  6.5 0.8 copy.11
  7.4 0.0 copy-start.2
  7.4 0.0 copy-start.3
  7.4 0.0 copy-start.4
  7.4 2.0 concatenate.3
  9.4 0.0 all-gather.2.cloned.1.call-update
  9.4 0.0 copy-done
  9.4 0.1 convert_reduce_fusion.4
  9.5 0.2 fusion.97
  9.8 233.1 %all-gather.2.cloned.1.call-done = bf16[2304,2049]{1,0:T(8,128)(2,1)} async-done(((bf16[96,2049]{1,0:T(8,128)(2,1)}), bf16[2304,2049]{1,0:T(8,128)(2,1)}) %all-gather.2.cloned.1.call-update) | async-done | bytes 9441808 | tf_op jit(solution)/shard_map/all_gather | solution.py:16
  242.8 1.3 convert_reduce_fusion
  244.1 0.0 copy-done.2
  244.2 0.0 copy-done.3
  244.2 0.0 copy-done.4
  244.2 0.0 copy-start.1
  244.2 7.0 %fusion.45 = bf16[128,1024]{1,0:T(8,128)(2,1)S(1)} fusion(bf16[2304,2049]{1,0:T(8,128)(2,1)} %all-gather.2.cloned.1.call-done, bf16[1,128,1024]{2,1,0:T(8,128)(2,1)S(1)} %copy-done, f32[2304]{0:T(1024)S(1)} %convert_reduce_fusion, f32[1024]{0:T(1024)S(1)} %bitcast.51, f32[1024]{0:T(1024)S(1)} %bitcast.55, f32[1024]{0:T(1024)S(1)} %bitcast.59, ...), kind=kOutput, calls=%fused_computation.27 | convolution fusion | flops 1211334656 | bytes 10249216 | tf_op jit(solution)/shard_map/dot_general | solution.py:56
  251.2 1.9 collective-permute-start
  253.1 0.0 copy-done.1
  253.1 0.7 fusion.149
  255.8 6.7 %collective-permute-done = bf16[128,1024]{1,0:T(8,128)(2,1)S(1)} collective-permute-done((bf16[128,1024]{1,0:T(8,128)(2,1)S(1)}, bf16[128,1024]{1,0:T(8,128)(2,1)S(1)}, u32[]{:S(2)}, u32[]{:S(2)}) %collective-permute-start) | collective-permute-done | bytes 262176 | tf_op jit(solution)/shard_map/ppermute | solution.py:27
  262.5 1.1 convert_reduce_fusion.3
  263.6 0.2 fusion.93
  263.8 7.0 %fusion.42 = bf16[128,1024]{1,0:T(8,128)(2,1)S(1)} fusion(bf16[2304,2049]{1,0:T(8,128)(2,1)} %all-gather.2.cloned.1.call-done, bf16[128,1024]{1,0:T(8,128)(2,1)S(1)} %get-tuple-element.10, f32[2304]{0:T(1024)S(1)} %convert_reduce_fusion, f32[128]{0:T(128)S(1)} %add_rsqrt_fusion.2, f32[128]{0:T(128)S(1)} %broadcast_multiply_fusion.2, f32[1024]{0:T(1024)S(1)} %bitcast.52, ...), kind=kOutput, calls=%fused_computation.26 | convolution fusion | flops 1211334656 | bytes 10249216 | tf_op jit(solution)/shard_map/dot_general | solution.py:56
  270.8 1.9 collective-permute-start.1
  274.6 7.5 %collective-permute-done.1 = bf16[128,1024]{1,0:T(8,128)(2,1)S(1)} collective-permute-done((bf16[128,1024]{1,0:T(8,128)(2,1)S(1)}, bf16[128,1024]{1,0:T(8,128)(2,1)S(1)}, u32[]{:S(2)}, u32[]{:S(2)}) %collective-permute-start.1) | collective-permute-done | bytes 262176 | tf_op jit(solution)/shard_map/ppermute | solution.py:27
  282.1 1.1 convert_reduce_fusion.2
  283.2 0.2 fusion.89
  283.4 7.0 %fusion.39 = bf16[128,1024]{1,0:T(8,128)(2,1)S(1)} fusion(bf16[2304,2049]{1,0:T(8,128)(2,1)} %all-gather.2.cloned.1.call-done, bf16[128,1024]{1,0:T(8,128)(2,1)S(1)} %get-tuple-element.8, f32[2304]{0:T(1024)S(1)} %convert_reduce_fusion, f32[128]{0:T(128)S(1)} %add_rsqrt_fusion.1, f32[128]{0:T(128)S(1)} %broadcast_multiply_fusion.1, f32[1024]{0:T(1024)S(1)} %bitcast.53, ...), kind=kOutput, calls=%fused_computation.25 | convolution fusion | flops 1211334656 | bytes 10249216 | tf_op jit(solution)/shard_map/dot_general | solution.py:56
  290.4 2.1 collective-permute-start.2
  294.5 7.3 %collective-permute-done.2 = bf16[128,1024]{1,0:T(8,128)(2,1)S(1)} collective-permute-done((bf16[128,1024]{1,0:T(8,128)(2,1)S(1)}, bf16[128,1024]{1,0:T(8,128)(2,1)S(1)}, u32[]{:S(2)}, u32[]{:S(2)}) %collective-permute-start.2) | collective-permute-done | bytes 262176 | tf_op jit(solution)/shard_map/ppermute | solution.py:27
  301.7 1.1 convert_reduce_fusion.1
  302.8 0.2 fusion.85
  303.1 7.0 %fusion.36 = bf16[128,1024]{1,0:T(8,128)(2,1)S(1)} fusion(bf16[2304,2049]{1,0:T(8,128)(2,1)} %all-gather.2.cloned.1.call-done, bf16[128,1024]{1,0:T(8,128)(2,1)S(1)} %get-tuple-element.6, f32[2304]{0:T(1024)S(1)} %convert_reduce_fusion, f32[128]{0:T(128)S(1)} %add_rsqrt_fusion, f32[128]{0:T(128)S(1)} %broadcast_multiply_fusion, f32[1024]{0:T(1024)S(1)} %bitcast.54, ...), kind=kOutput, calls=%fused_computation.24 | convolution fusion | flops 1211334656 | bytes 10249216 | tf_op jit(solution)/shard_map/dot_general | solution.py:56
  310.0 1.9 collective-permute-start.3
  312.0 9.4 %collective-permute-done.3 = bf16[128,1024]{1,0:T(8,128)(2,1)S(1)} collective-permute-done((bf16[128,1024]{1,0:T(8,128)(2,1)S(1)}, bf16[128,1024]{1,0:T(8,128)(2,1)S(1)}, u32[]{:S(2)}, u32[]{:S(2)}) %collective-permute-start.3) | collective-permute-done | bytes 262176 | tf_op jit(solution)/shard_map/ppermute | solution.py:27
  321.3 1.1 maximum_bitcast_fusion
  (8 shorter events, 0.1 us)
Async XLA Ops:
  6.5 2.9 copy-start
  6.5 236.3 %all-gather.2.cloned.1.call-start = ((), (), s32[]{:S(2)}) async-start(), calls=%async_computation | async-start | bytes 10444800 | tf_op jit(solution)/shard_map/all_gather | solution.py:16
  7.4 236.8 %copy-start.2 = (f32[1,1024]{1,0:T(1,128)S(1)}, f32[1,1024]{1,0:T(1,128)}, u32[]{:S(2)}) copy-start(f32[1,1024]{1,0:T(1,128)} %param.13) | copy-start | bytes 12292
  7.4 236.8 %copy-start.3 = (f32[1,1024]{1,0:T(1,128)S(1)}, f32[1,1024]{1,0:T(1,128)}, u32[]{:S(2)}) copy-start(f32[1,1024]{1,0:T(1,128)} %param.15) | copy-start | bytes 12292
  7.4 236.8 %copy-start.4 = (f32[1,1024]{1,0:T(1,128)S(1)}, f32[1,1024]{1,0:T(1,128)}, u32[]{:S(2)}) copy-start(f32[1,1024]{1,0:T(1,128)} %param.14) | copy-start | bytes 12292
  244.2 8.9 %copy-start.1 = (s32[3]{0:T(128)S(1)}, s32[3]{0:T(128)}, u32[]{:S(2)}) copy-start(s32[3]{0:T(128)} %param.17) | copy-start | bytes 40
  251.2 11.3 %collective-permute-start = (bf16[128,1024]{1,0:T(8,128)(2,1)S(1)}, bf16[128,1024]{1,0:T(8,128)(2,1)S(1)}, u32[]{:S(2)}, u32[]{:S(2)}) collective-permute-start(bf16[128,1024]{1,0:T(8,128)(2,1)S(1)} %fusion.45), channel_id=1, source_target_pairs={{0,24},{24,48},{48,72},{72,96},{96,120},{120,144},{144,168},{168,1... | collective-permute-start | bytes 786440 | tf_op jit(solution)/shard_map/ppermute | solution.py:27
  270.8 11.3 %collective-permute-start.1 = (bf16[128,1024]{1,0:T(8,128)(2,1)S(1)}, bf16[128,1024]{1,0:T(8,128)(2,1)S(1)}, u32[]{:S(2)}, u32[]{:S(2)}) collective-permute-start(bf16[128,1024]{1,0:T(8,128)(2,1)S(1)} %fusion.42), channel_id=1, source_target_pairs={{0,24},{24,48},{48,72},{72,96},{96,120},{120,144},{144,168},{168,1... | collective-permute-start | bytes 786440 | tf_op jit(solution)/shard_map/ppermute | solution.py:27
  290.4 11.3 %collective-permute-start.2 = (bf16[128,1024]{1,0:T(8,128)(2,1)S(1)}, bf16[128,1024]{1,0:T(8,128)(2,1)S(1)}, u32[]{:S(2)}, u32[]{:S(2)}) collective-permute-start(bf16[128,1024]{1,0:T(8,128)(2,1)S(1)} %fusion.39), channel_id=1, source_target_pairs={{0,24},{24,48},{48,72},{72,96},{96,120},{120,144},{144,168},{168,1... | collective-permute-start | bytes 786440 | tf_op jit(solution)/shard_map/ppermute | solution.py:27
  310.0 11.3 %collective-permute-start.3 = (bf16[128,1024]{1,0:T(8,128)(2,1)S(1)}, bf16[128,1024]{1,0:T(8,128)(2,1)S(1)}, u32[]{:S(2)}, u32[]{:S(2)}) collective-permute-start(bf16[128,1024]{1,0:T(8,128)(2,1)S(1)} %fusion.36), channel_id=1, source_target_pairs={{0,24},{24,48},{48,72},{72,96},{96,120},{120,144},{144,168},{168,1... | collective-permute-start | bytes 786440 | tf_op jit(solution)/shard_map/ppermute | solution.py:27
Sparse Core Ops, SparseCore 0:
  9.7 233.0 all-gather.1
where the time goes:
time: 330 us; the launch traced here: 329 us
  waiting for transfers between devices  264 us (80%)
  matrix products  27.9 us (8%)
  between operations  19.4 us (6%)
  starting transfers between devices  7.86 us (2%)
  other arithmetic  6.79 us (2%)
  local copies, waits for them, and re-layouts  3.5 us (1%)
    all_gather x1, waiting for transfers between devices, side_by_side(): out, at, outs = (lax.all_gather(both, axis, axis=dim, tiled=True), 0, [])  233 us
    ppermute x4, waiting for transfers between devices, passed_along(): return lax.ppermute(value, axis, pairs)  30.8 us
    dot_general x4, matrix products, apply_block(): jnp.dot(hidden, full_out, preferred_element_type=jnp.float32)  27.9 us
    ppermute x4, starting transfers between devices, passed_along(): return lax.ppermute(value, axis, pairs)  7.86 us
  transfers between devices with their start and end apart: 5, of which 5 were waited for; matrix products, arithmetic and copies ran while one was open for 0% of the time, Pallas kernels for 0%

commit v1 on v0

v1 whole, which is shorter than its diff:
```python
import functools

import jax
import jax.numpy as jnp
from jax import lax
from jax.experimental import pallas as pl
from jax.experimental.pallas import tpu as pltpu
from jax.sharding import PartitionSpec as P

TICKS = 4
CHUNKS = 2
MESH = pl.DeviceIdType.MESH

norm_floor = 0.1
gelu_slope = 1.702

BIAS, W_IN, W_OUT = 0, 1, 2


def normalize(current, gain_row, shift_row):
    widened = current.astype(jnp.float32)
    average = jnp.mean(widened, axis=-1, keepdims=True)
    centered = widened - average
    variance = jnp.mean(centered * centered, axis=-1, keepdims=True)
    normed = (centered * lax.rsqrt(variance + norm_floor) * gain_row + shift_row).astype(
        jnp.bfloat16
    )
    return (normed, widened)


def activate(preact):
    return preact * jax.nn.sigmoid(gelu_slope * preact)


def rows_times(normed, rows):
    return lax.dot_general(
        normed, rows, (((1,), (1,)), ((), ())), preferred_element_type=jnp.float32
    )


def block_kernel(
    yn, zn,
    x_in, w_in, w_out, small_in, patches_in, plan, out,
    x0, win, wout, small, bias, bias_row, pat, sel, sel_far, cur, normed0, acc, hid, prod, arr,
    own_sem, own_send, ring_send, ring_recv, core_send, core_recv,
    pat_sem, sel_send, sel_recv, hop_send, hop_recv, back_send, back_recv,
):
    section = lax.axis_index("section")
    tensor = lax.axis_index("tensor")
    k = lax.rem(section, 2)
    y = lax.div(section, 2)
    r = lax.rem(tensor, 2)
    z = lax.div(tensor, 2)
    tokens, depth = x0.shape
    shard = w_in.shape[1]
    width = win.shape[0]
    half = zn // 2
    rows = tokens // CHUNKS

    def device(y, k, z, r):
        return (2 * y + k, 2 * z + r)

    up = device(y, k, lax.rem(z + 1, zn), r)
    down = device(y, k, lax.rem(z + zn - 1, zn), r)
    sibling = device(y, 1 - k, z, r)
    swapped = device(y, r, z, k)
    after = device(lax.rem(y + r, yn), k, z, 1 - r)
    before = device(lax.rem(y + yn - 1 + r, yn), k, z, 1 - r)
    last_to = device(lax.rem(y + r, yn), 1 - r, z, k)
    last_from = device(lax.rem(y + yn - 1 + k, yn), r, z, 1 - k)
    stays = r == k
    moves = r != k

    def slot_ref(piece, slot):
        if piece == BIAS:
            return bias.at[slot]
        whole = win if piece == W_IN else wout
        return whole.at[pl.ds(pl.multiple_of(slot * shard, shard), shard)]

    own = 2 * z + k
    sources = (small_in.at[:, pl.ds(0, 128)], w_in.at[0], w_out.at[0], small_in, x_in.at[0])

    def own_targets(slot):
        return (slot_ref(BIAS, slot), slot_ref(W_IN, slot), slot_ref(W_OUT, slot), small, x0)

    def own_local(i):
        return pltpu.make_async_copy(sources[i], own_targets(own)[i], own_sem.at[i])

    def own_remote(i, slot):
        return pltpu.make_async_remote_copy(
            src_ref=sources[i],
            dst_ref=own_targets(slot)[i],
            send_sem=own_send.at[i],
            recv_sem=own_sem.at[i],
            device_id=swapped,
            device_id_type=MESH,
        )

    def own_wait(i):
        @pl.when(stays)
        def _():
            own_local(i).wait()

        @pl.when(moves)
        def _():
            own_remote(i, own).wait_recv()

    def patch_load():
        return pltpu.make_async_copy(patches_in, pat, pat_sem.at[0])

    @pl.when(stays)
    def _():
        for i in range(5):
            own_local(i).start()

    @pl.when(section == 0)
    def _():
        patch_load().start()

    barrier = pltpu.get_barrier_semaphore()

    def greet(partner):
        pl.semaphore_signal(barrier, inc=1, device_id=partner, device_id_type=MESH)

    for partner in (up, down, sibling, after, before):
        greet(partner)

    @pl.when(r + k > 0)
    def _():
        greet(last_to)

    @pl.when(r + 1 - k > 0)
    def _():
        greet(last_from)

    @pl.when(moves)
    def _():
        greet(swapped)

    pl.semaphore_wait(barrier, 6 + r + lax.rem(r + k, 2))

    @pl.when(moves)
    def _():
        for i in range(5):
            own_remote(i, 2 * z + r).start()

    def hops(way, piece):
        return half if (piece == W_OUT) == (way == 1) else half - 1

    def ring(way, hop, piece, arriving):
        distance = hop + 1 if arriving else hop
        place = lax.rem(z + (zn - distance if way == 0 else distance), zn)
        ref = slot_ref(piece, 2 * place + k)
        return pltpu.make_async_remote_copy(
            src_ref=ref,
            dst_ref=ref,
            send_sem=ring_send.at[way, hop, piece],
            recv_sem=ring_recv.at[way, hop, piece],
            device_id=up if way == 0 else down,
            device_id_type=MESH,
        )

    def across(offset, piece, arriving):
        place = lax.rem(z + offset, zn)
        ref = slot_ref(piece, 2 * place + (1 - k if arriving else k))
        return pltpu.make_async_remote_copy(
            src_ref=ref,
            dst_ref=ref,
            send_sem=core_send.at[offset, piece],
            recv_sem=core_recv.at[offset, piece],
            device_id=sibling,
            device_id_type=MESH,
        )

    for piece in (BIAS, W_IN, W_OUT):
        own_wait(piece)
        ring(0, 0, piece, False).start()
        ring(1, 0, piece, False).start()
        across(0, piece, False).start()

    own_wait(3)
    own_wait(4)
    gain_row = small[1:2, 128:]
    shift_row = small[2:3, 128:]
    out_row = small[0:1, 128:]
    normed, widened = normalize(x0[...], gain_row, shift_row)
    normed0[...] = normed
    acc[...] = widened + out_row

    def add_shard(slot):
        at = pl.ds(pl.multiple_of(slot * shard, shard), shard)
        preact = rows_times(normed0[...], win[at, :]) + bias[slot][0:1, :shard]
        hidden = activate(preact).astype(jnp.bfloat16)
        acc[...] += jnp.dot(hidden, wout[at, :], preferred_element_type=jnp.float32)

    def add_offset(offset):
        for piece in (BIAS, W_IN, W_OUT):
            across(offset, piece, True).wait_recv()
        place = lax.rem(z + offset, zn)
        add_shard(2 * place)
        add_shard(2 * place + 1)

    def take(hop, piece):
        for way in (0, 1):
            if hop < hops(way, piece):
                ring(way, hop, piece, True).wait_recv()
                if hop + 1 < hops(way, piece):
                    ring(way, hop + 1, piece, False).start()
                across((zn - hop - 1 if way == 0 else hop + 1) % zn, piece, False).start()

    def select_send():
        return pltpu.make_async_remote_copy(
            src_ref=sel,
            dst_ref=sel_far,
            send_sem=sel_send.at[0],
            recv_sem=sel_recv.at[0],
            device_id=swapped,
            device_id_type=MESH,
        )

    for hop in range(half):
        take(hop, BIAS)
        take(hop, W_IN)
        add_offset((zn - hop) % zn)
        take(hop, W_OUT)
        if hop:
            add_offset(hop)
        else:

            @pl.when(section == 0)
            def _():
                patch_load().wait()
                for i in range(TICKS - 1):
                    sel[i] = pat[plan[i]]

            @pl.when((section == 0) & (r == 1))
            def _():
                select_send().start()

    add_offset(half)

    @pl.when((section == 1) & (r == 0))
    def _():
        select_send().wait_recv()

    for first in range(0, 2 * zn, 4):
        bias_row[0:1, pl.ds(first * shard, 4 * shard)] = jnp.concatenate(
            [bias[slot][0:1, :shard] for slot in range(first, first + 4)], axis=1
        )

    def chunk_rows(chunk):
        return pl.ds(chunk * rows, rows)

    def hop_on(tick, chunk):
        at = chunk_rows(chunk)
        return pltpu.make_async_remote_copy(
            src_ref=prod.at[tick, at],
            dst_ref=arr.at[tick, at],
            send_sem=hop_send.at[tick, chunk],
            recv_sem=hop_recv.at[tick, chunk],
            device_id=after,
            device_id_type=MESH,
        )

    def hop_last(chunk):
        at = chunk_rows(chunk)
        return pltpu.make_async_remote_copy(
            src_ref=prod.at[TICKS - 1, at],
            dst_ref=out.at[0, TICKS - 1, at],
            send_sem=hop_send.at[TICKS - 1, chunk],
            recv_sem=hop_recv.at[TICKS - 1, chunk],
            device_id=last_to,
            device_id_type=MESH,
        )

    def record_local(tick, chunk):
        at = chunk_rows(chunk)
        return pltpu.make_async_copy(
            arr.at[tick, at], out.at[0, tick, at], back_recv.at[tick, chunk]
        )

    def record_remote(tick, chunk):
        at = chunk_rows(chunk)
        return pltpu.make_async_remote_copy(
            src_ref=arr.at[tick, at],
            dst_ref=out.at[0, tick, at],
            send_sem=back_send.at[tick, chunk],
            recv_sem=back_recv.at[tick, chunk],
            device_id=swapped,
            device_id_type=MESH,
        )

    prod[0] = acc[...].astype(jnp.bfloat16)
    for chunk in range(CHUNKS):
        hop_on(0, chunk).start()

    wide = 256

    def step(tick, chunk):
        at = chunk_rows(chunk)
        hop_on(tick - 1, chunk).wait_recv()

        @pl.when(stays)
        def _():
            record_local(tick - 1, chunk).start()

        @pl.when(moves)
        def _():
            record_remote(tick - 1, chunk).start()

        cur[...] = arr[tick - 1, at, :]

        @pl.when((section == 0) & (r == 0))
        def _():
            cur[...] = sel[tick - 1, at, :]

        @pl.when((section == 1) & (r == 0))
        def _():
            cur[...] = sel_far[tick - 1, at, :]

        normed, widened = normalize(cur[...], gain_row, shift_row)
        for low in range(0, width, wide):
            preact = rows_times(normed, win[low : low + wide, :]) + bias_row[0:1, low : low + wide]
            hid[:, low : low + wide] = activate(preact).astype(jnp.bfloat16)
        for low in range(0, depth, wide):
            mixed = jnp.dot(
                hid[...], wout[:, low : low + wide], preferred_element_type=jnp.float32
            )
            prod[tick, at, low : low + wide] = (
                widened[:, low : low + wide] + mixed + out_row[:, low : low + wide]
            ).astype(jnp.bfloat16)

        @pl.when(tick < TICKS - 1)
        def _():
            hop_on(tick, chunk).start()

        @pl.when(tick == TICKS - 1)
        def _():
            hop_last(chunk).start()

    @pl.loop(1, TICKS)
    def _(tick):
        for chunk in range(CHUNKS):
            step(tick, chunk)

    for tick in range(TICKS - 1):
        for chunk in range(CHUNKS):

            @pl.when(stays)
            def _():
                record_local(tick, chunk).wait()

            @pl.when(moves)
            def _():
                record_remote(tick, chunk).wait_recv()
                record_remote(tick, chunk).wait_send()

            hop_on(tick, chunk).wait_send()

    @pl.when(moves)
    def _():
        for i in range(5):
            own_remote(i, 2 * z + r).wait_send()

    @pl.when((section == 0) & (r == 1))
    def _():
        select_send().wait_send()

    for piece in (BIAS, W_IN, W_OUT):
        for way in (0, 1):
            for hop in range(hops(way, piece)):
                ring(way, hop, piece, False).wait_send()
        for offset in range(zn):
            across(offset, piece, False).wait_send()
    for chunk in range(CHUNKS):
        hop_last(chunk).wait_send()
        hop_last(chunk).wait_recv()


def shards(
    section_inputs, w_in, in_bias, w_out, out_bias, norm_gain, norm_bias, patches, plan, *, yn, zn
):
    tokens, depth = section_inputs.shape[1:]
    shard = w_in.shape[1]
    width = 2 * zn * shard
    lanes = -shard % 128
    small = jnp.concatenate(
        [
            jnp.pad(in_bias.astype(jnp.float32), ((0, 7), (0, lanes))),
            jnp.pad(jnp.concatenate([out_bias, norm_gain, norm_bias]), ((0, 5), (0, 0))),
        ],
        axis=1,
    )
    anywhere = pl.BlockSpec(memory_space=pl.ANY)
    half = zn // 2
    dma = pltpu.SemaphoreType.DMA
    return pl.pallas_call(
        functools.partial(block_kernel, yn, zn),
        out_shape=jax.ShapeDtypeStruct((1, TICKS, tokens, depth), jnp.bfloat16),
        in_specs=[anywhere] * 5 + [pl.BlockSpec(memory_space=pltpu.SMEM)],
        out_specs=anywhere,
        scratch_shapes=[
            pltpu.VMEM((tokens, depth), jnp.bfloat16),
            pltpu.VMEM((width, depth), jnp.bfloat16),
            pltpu.VMEM((width, depth), jnp.bfloat16),
            pltpu.VMEM(small.shape, jnp.float32),
            pltpu.VMEM((2 * zn, 8, 128), jnp.float32),
            pltpu.VMEM((8, width), jnp.float32),
            pltpu.VMEM(patches.shape, jnp.bfloat16),
            pltpu.VMEM((TICKS - 1, tokens, depth), jnp.bfloat16),
            pltpu.VMEM((TICKS - 1, tokens, depth), jnp.bfloat16),
            pltpu.VMEM((tokens // CHUNKS, depth), jnp.bfloat16),
            pltpu.VMEM((tokens, depth), jnp.bfloat16),
            pltpu.VMEM((tokens, depth), jnp.float32),
            pltpu.VMEM((tokens // CHUNKS, width), jnp.bfloat16),
            pltpu.VMEM((TICKS, tokens, depth), jnp.bfloat16),
            pltpu.VMEM((TICKS - 1, tokens, depth), jnp.bfloat16),
            dma((5,)),
            dma((5,)),
            dma((2, half, 3)),
            dma((2, half, 3)),
            dma((2 * half, 3)),
            dma((2 * half, 3)),
            dma((1,)),
            dma((1,)),
            dma((1,)),
            dma((TICKS, CHUNKS)),
            dma((TICKS, CHUNKS)),
            dma((TICKS - 1, CHUNKS)),
            dma((TICKS - 1, CHUNKS)),
        ],
        compiler_params=pltpu.CompilerParams(collective_id=0, has_side_effects=True),
    )(section_inputs, w_in, w_out, small, patches, plan)


def solution(mesh):
    placed = (
        P("section", "tensor", None),
        P("section", "tensor", None),
        P("section", "tensor"),
        P("section", "tensor", None),
        P("section", None),
        P("section", None),
        P("section", None),
        P(None, "tensor", None),
        P(),
    )
    return jax.shard_map(
        functools.partial(
            shards, yn=mesh.shape["section"] // 2, zn=mesh.shape["tensor"] // 2
        ),
        mesh=mesh,
        in_specs=placed,
        out_specs=P("section", None, "tensor", None),
        check_vma=False,
    )
```

time: 330 us -> 110 us (0.33)
  the two profiles are of different devices: /device:TPU:66 before, /device:TPU:1 now
where the time goes in v1:
time: 110 us; the launch traced here: 108 us
  Pallas kernels  103 us (94%)
  local copies, waits for them, and re-layouts  2.26 us (2%)
  other arithmetic  2.02 us (2%)
    pallas_call x1, Pallas kernels, shards(): pl.pallas_call(functools.partial(block_kernel, yn, zn), out_shape=jax.Sha...  103 us
    unnamed x1, local copies, waits for them, and re-layouts  2.26 us

profile of v1, /device:TPU:1, one launch (start us, length us, event | category | flops | bytes accessed | tf_op | source)
XLA Modules:
  0.0 107.6 jit_solution(8617085537171159792)
XLA Ops:
  0.0 0.7 pad_convert_fusion
  0.7 0.7 select_maximum_fusion
  1.4 0.6 pad_maximum_fusion.small_in
  2.0 103.3 %shard_map.91 = bf16[1,4,128,1024]{3,2,1,0:T(8,128)(2,1)} custom-call(bf16[1,128,1024]{2,1,0:T(8,128)(2,1)} %x_in.1, bf16[1,96,1024]{2,1,0:T(8,128)(2,1)} %w_in.1, bf16[1,96,1024]{2,1,0:T(8,128)(2,1)} %w_out.1, f32[8,1152]{1,0:T(8,128)} %pad_maximum_fusion.small_in, bf16[8,128,1024]{2,1,0:T(8,128)(2,1)} %patches_in.1, s32[3]{0:T(128)} %plan.1), custom_call_target="tpu_custom_call" | custom-call | tf_op jit(solution)/shard_map/pallas_call | solution.py:397
  105.3 2.3 %copy.11 = bf16[1,4,128,1024]{3,2,1,0:T(8,128)(2,1)} copy(bf16[1,4,128,1024]{3,2,1,0:T(8,128)(2,1)} %shard_map.91) | data formatting | bytes 2097152

commit v2 on v1

--- a/solution.py
+++ b/solution.py
@@ -14,7 +14,7 @@
 norm_floor = 0.1
 gelu_slope = 1.702
 
-BIAS, W_IN, W_OUT = 0, 1, 2
+PIECES = 5
 
 
 def normalize(current, gain_row, shift_row):
@@ -62,6 +62,7 @@
 
     up = device(y, k, lax.rem(z + 1, zn), r)
     down = device(y, k, lax.rem(z + zn - 1, zn), r)
+    onward = device(y, k, lax.rem(z + 1 + k * (zn - 2), zn), r)
     sibling = device(y, 1 - k, z, r)
     swapped = device(y, r, z, k)
     after = device(lax.rem(y + r, yn), k, z, 1 - r)
@@ -71,17 +72,28 @@
     stays = r == k
     moves = r != k
 
+    part = shard // 2
+
     def slot_ref(piece, slot):
-        if piece == BIAS:
+        if piece == 0:
             return bias.at[slot]
-        whole = win if piece == W_IN else wout
-        return whole.at[pl.ds(pl.multiple_of(slot * shard, shard), shard)]
+        whole = win if piece < 3 else wout
+        first = slot * shard + (piece + 1) % 2 * part
+        return whole.at[pl.ds(pl.multiple_of(first, part), part)]
 
     own = 2 * z + k
-    sources = (small_in.at[:, pl.ds(0, 128)], w_in.at[0], w_out.at[0], small_in, x_in.at[0])
+    sources = (
+        small_in.at[:, pl.ds(0, 128)],
+        w_in.at[0, pl.ds(0, part)],
+        w_in.at[0, pl.ds(part, part)],
+        w_out.at[0, pl.ds(0, part)],
+        w_out.at[0, pl.ds(part, part)],
+        small_in,
+        x_in.at[0],
+    )
 
     def own_targets(slot):
-        return (slot_ref(BIAS, slot), slot_ref(W_IN, slot), slot_ref(W_OUT, slot), small, x0)
+        return tuple(slot_ref(piece, slot) for piece in range(PIECES)) + (small, x0)
 
     def own_local(i):
         return pltpu.make_async_copy(sources[i], own_targets(own)[i], own_sem.at[i])
@@ -110,7 +122,7 @@
 
     @pl.when(stays)
     def _():
-        for i in range(5):
+        for i in range(PIECES + 2):
             own_local(i).start()
 
     @pl.when(section == 0)
@@ -141,45 +153,56 @@
 
     @pl.when(moves)
     def _():
-        for i in range(5):
+        for i in range(PIECES + 2):
             own_remote(i, 2 * z + r).start()
 
-    def hops(way, piece):
-        return half if (piece == W_OUT) == (way == 1) else half - 1
-
-    def ring(way, hop, piece, arriving):
-        distance = hop + 1 if arriving else hop
-        place = lax.rem(z + (zn - distance if way == 0 else distance), zn)
-        ref = slot_ref(piece, 2 * place + k)
+    first_stream = (r, 1 - r)
+
+    def place_at(distance):
+        return lax.rem(z + lax.rem(k * 2 * distance + zn - distance, zn), zn)
+
+    def ring(hop, i, piece, arriving):
+        ref = slot_ref(piece, 2 * place_at(hop + 1 if arriving else hop) + first_stream[i])
         return pltpu.make_async_remote_copy(
             src_ref=ref,
             dst_ref=ref,
-            send_sem=ring_send.at[way, hop, piece],
-            recv_sem=ring_recv.at[way, hop, piece],
-            device_id=up if way == 0 else down,
-            device_id_type=MESH,
-        )
-
-    def across(offset, piece, arriving):
-        place = lax.rem(z + offset, zn)
-        ref = slot_ref(piece, 2 * place + (1 - k if arriving else k))
+            send_sem=ring_send.at[hop, i, piece],
+            recv_sem=ring_recv.at[hop, i, piece],
+            device_id=onward,
+            device_id_type=MESH,
+        )
+
+    def across(distance, i, piece, arriving):
+        place = place_at((zn - distance) % zn if arriving else distance)
+        ref = slot_ref(piece, 2 * place + first_stream[i])
         return pltpu.make_async_remote_copy(
             src_ref=ref,
             dst_ref=ref,
-            send_sem=core_send.at[offset, piece],
-            recv_sem=core_recv.at[offset, piece],
+            send_sem=core_send.at[distance, i, piece],
+            recv_sem=core_recv.at[distance, i, piece],
             device_id=sibling,
             device_id_type=MESH,
         )
 
-    for piece in (BIAS, W_IN, W_OUT):
-        own_wait(piece)
-        ring(0, 0, piece, False).start()
-        ring(1, 0, piece, False).start()
-        across(0, piece, False).start()
-
-    own_wait(3)
-    own_wait(4)
+    def farthest(arriving):
+        return [(k == (1 if arriving else 0), range(0, 3)), (k == (0 if arriving else 1), range(3, 5))]
+
+    for i, mine in ((0, stays), (1, moves)):
+        for piece in range(PIECES):
+
+            @pl.when(mine)
+            def _():
+                own_wait(piece)
+                across(0, i, piece, False).start()
+
+            @pl.when(jnp.logical_not(mine))
+            def _():
+                across(0, i, piece, True).wait_recv()
+
+            ring(0, i, piece, False).start()
+
+    own_wait(PIECES)
+    own_wait(PIECES + 1)
     gain_row = small[1:2, 128:]
     shift_row = small[2:3, 128:]
     out_row = small[0:1, 128:]
@@ -187,26 +210,52 @@
     normed0[...] = normed
     acc[...] = widened + out_row
 
-    def add_shard(slot):
-        at = pl.ds(pl.multiple_of(slot * shard, shard), shard)
-        preact = rows_times(normed0[...], win[at, :]) + bias[slot][0:1, :shard]
-        hidden = activate(preact).astype(jnp.bfloat16)
+    def add_place(place):
+        at = pl.ds(pl.multiple_of(place * 2 * shard, 2 * shard), 2 * shard)
+        both = jnp.concatenate(
+            [bias[2 * place][0:1, :shard], bias[2 * place + 1][0:1, :shard]], axis=1
+        )
+        hidden = activate(rows_times(normed0[...], win[at, :]) + both).astype(jnp.bfloat16)
         acc[...] += jnp.dot(hidden, wout[at, :], preferred_element_type=jnp.float32)
 
-    def add_offset(offset):
-        for piece in (BIAS, W_IN, W_OUT):
-            across(offset, piece, True).wait_recv()
-        place = lax.rem(z + offset, zn)
-        add_shard(2 * place)
-        add_shard(2 * place + 1)
-
-    def take(hop, piece):
-        for way in (0, 1):
-            if hop < hops(way, piece):
-                ring(way, hop, piece, True).wait_recv()
-                if hop + 1 < hops(way, piece):
-                    ring(way, hop + 1, piece, False).start()
-                across((zn - hop - 1 if way == 0 else hop + 1) % zn, piece, False).start()
+    def take(hop):
+        for i in (0, 1):
+            for piece in range(PIECES):
+                ring(hop, i, piece, True).wait_recv()
+                if hop + 2 < half:
+                    ring(hop + 1, i, piece, False).start()
+                across(hop + 1, i, piece, False).start()
+            if hop + 2 == half:
+                for here, pieces in farthest(False):
+
+                    @pl.when(here)
+                    def _():
+                        for piece in pieces:
+                            ring(hop + 1, i, piece, False).start()
+
+    def take_farthest():
+        for here, pieces in farthest(False):
+
+            @pl.when(here)
+            def _():
+                for i in (0, 1):
+                    for piece in pieces:
+                        ring(half - 1, i, piece, True).wait_recv()
+                        across(half, i, piece, False).start()
+
+    def given(distance):
+        for i in (0, 1):
+            for piece in range(PIECES):
+                across(distance, i, piece, True).wait_recv()
+
+    def given_farthest():
+        for here, pieces in farthest(True):
+
+            @pl.when(here)
+            def _():
+                for i in (0, 1):
+                    for piece in pieces:
+                        across(half, i, piece, True).wait_recv()
 
     def select_send():
         return pltpu.make_async_remote_copy(
@@ -218,14 +267,11 @@
             device_id_type=MESH,
         )
 
-    for hop in range(half):
-        take(hop, BIAS)
-        take(hop, W_IN)
-        add_offset((zn - hop) % zn)
-        take(hop, W_OUT)
-        if hop:
-            add_offset(hop)
-        else:
+    add_place(z)
+    for hop in range(half - 1):
+        take(hop)
+        add_place(place_at(hop + 1))
+        if hop == 1:
 
             @pl.when(section == 0)
             def _():
@@ -237,7 +283,15 @@
             def _():
                 select_send().start()
 
-    add_offset(half)
+        if hop >= 2:
+            given(hop - 1)
+            add_place(place_at(zn - hop + 1))
+    for distance in range(max(1, half - 2), half):
+        given(distance)
+        add_place(place_at(zn - distance))
+    take_farthest()
+    given_farthest()
+    add_place(place_at(half))
 
     @pl.when((section == 1) & (r == 0))
     def _():
@@ -359,19 +413,31 @@
 
     @pl.when(moves)
     def _():
-        for i in range(5):
+        for i in range(PIECES + 2):
             own_remote(i, 2 * z + r).wait_send()
 
     @pl.when((section == 0) & (r == 1))
     def _():
         select_send().wait_send()
 
-    for piece in (BIAS, W_IN, W_OUT):
-        for way in (0, 1):
-            for hop in range(hops(way, piece)):
-                ring(way, hop, piece, False).wait_send()
-        for offset in range(zn):
-            across(offset, piece, False).wait_send()
+    for i, mine in ((0, stays), (1, moves)):
+        for piece in range(PIECES):
+
+            @pl.when(mine)
+            def _():
+                across(0, i, piece, False).wait_send()
+
+            for hop in range(half - 1):
+                ring(hop, i, piece, False).wait_send()
+                across(hop + 1, i, piece, False).wait_send()
+        for here, pieces in farthest(False):
+
+            @pl.when(here)
+            def _():
+                for piece in pieces:
+                    ring(half - 1, i, piece, False).wait_send()
+                    across(half, i, piece, False).wait_send()
+
     for chunk in range(CHUNKS):
         hop_last(chunk).wait_send()
         hop_last(chunk).wait_recv()
@@ -415,12 +481,12 @@
             pltpu.VMEM((tokens // CHUNKS, width), jnp.bfloat16),
             pltpu.VMEM((TICKS, tokens, depth), jnp.bfloat16),
             pltpu.VMEM((TICKS - 1, tokens, depth), jnp.bfloat16),
-            dma((5,)),
-            dma((5,)),
-            dma((2, half, 3)),
-            dma((2, half, 3)),
-            dma((2 * half, 3)),
-            dma((2 * half, 3)),
+            dma((PIECES + 2,)),
+            dma((PIECES + 2,)),
+            dma((half, 2, PIECES)),
+            dma((half, 2, PIECES)),
+            dma((half + 1, 2, PIECES)),
+            dma((half + 1, 2, PIECES)),
             dma((1,)),
             dma((1,)),
             dma((1,)),

time: 110 us -> 109 us (level); the launches traced: 108 us -> 108 us
  no operation moved by 1% of the time
where the time goes in v2:
time: 109 us; the launch traced here: 108 us
  Pallas kernels  104 us (95%)
  local copies, waits for them, and re-layouts  2.26 us (2%)
  other arithmetic  2.02 us (2%)
    pallas_call x1, Pallas kernels, shards(): pl.pallas_call(functools.partial(block_kernel, yn, zn), out_shape=jax.Sha...  104 us
    unnamed x1, local copies, waits for them, and re-layouts  2.26 us

profile of v2, /device:TPU:1, one launch (start us, length us, event | category | flops | bytes accessed | tf_op | source)
XLA Modules:
  0.0 108.5 jit_solution(9876260864055368512)
XLA Ops:
  0.0 0.7 pad_convert_fusion
  0.7 0.7 select_maximum_fusion
  1.4 0.6 pad_maximum_fusion.small_in
  2.0 104.2 %shard_map.91 = bf16[1,4,128,1024]{3,2,1,0:T(8,128)(2,1)} custom-call(bf16[1,128,1024]{2,1,0:T(8,128)(2,1)} %x_in.1, bf16[1,96,1024]{2,1,0:T(8,128)(2,1)} %w_in.1, bf16[1,96,1024]{2,1,0:T(8,128)(2,1)} %w_out.1, f32[8,1152]{1,0:T(8,128)} %pad_maximum_fusion.small_in, bf16[8,128,1024]{2,1,0:T(8,128)(2,1)} %patches_in.1, s32[3]{0:T(128)} %plan.1), custom_call_target="tpu_custom_call" | custom-call | tf_op jit(solution)/shard_map/pallas_call | solution.py:463
  106.2 2.3 %copy.11 = bf16[1,4,128,1024]{3,2,1,0:T(8,128)(2,1)} copy(bf16[1,4,128,1024]{3,2,1,0:T(8,128)(2,1)} %shard_map.91) | data formatting | bytes 2097152

commit v3 on v2

v3 whole, which is shorter than its diff:
```python
import functools

import jax
import jax.numpy as jnp
from jax import lax
from jax.experimental import pallas as pl
from jax.experimental.pallas import tpu as pltpu
from jax.sharding import PartitionSpec as P

TICKS = 4
CHUNKS = 2
MESH = pl.DeviceIdType.MESH

norm_floor = 0.1
gelu_slope = 1.702

OWN = 9
PIECES = 5


def normalize(current, gain_row, shift_row):
    widened = current.astype(jnp.float32)
    average = jnp.mean(widened, axis=-1, keepdims=True)
    centered = widened - average
    variance = jnp.mean(centered * centered, axis=-1, keepdims=True)
    normed = (centered * lax.rsqrt(variance + norm_floor) * gain_row + shift_row).astype(
        jnp.bfloat16
    )
    return (normed, widened)


def activate(preact):
    return preact * jax.nn.sigmoid(gelu_slope * preact)


def rows_times(normed, rows):
    return lax.dot_general(
        normed, rows, (((1,), (1,)), ((), ())), preferred_element_type=jnp.float32
    )


def block_kernel(
    yn, zn,
    x_in, w_in, w_out, bias_in, add_in, gain_in, shift_in, patches_in, plan, out,
    x0, win, wout, add, gain, shift, bias, bias_row, pat, sel, sel_far, cur, normed0, acc, hid, prod, arr,
    own_sem, own_send, ring_send, ring_recv, core_send, core_recv,
    pat_sem, sel_send, sel_recv, hop_send, hop_recv, record_send, record_recv,
):
    section = lax.axis_index("section")
    tensor = lax.axis_index("tensor")
    k = lax.rem(section, 2)
    y = lax.div(section, 2)
    r = lax.rem(tensor, 2)
    z = lax.div(tensor, 2)
    tokens, depth = x0.shape
    shard = w_in.shape[1]
    width = win.shape[0]
    near = (zn - 1) // 2
    rows = tokens // CHUNKS

    def device(y, k, z, r):
        return (2 * y + k, 2 * z + r)

    onward = device(y, k, lax.rem(z + 1 + k * (zn - 2), zn), r)
    inward = device(y, k, lax.rem(z + zn - 1 - k * (zn - 2), zn), r)
    sibling = device(y, 1 - k, z, r)
    swapped = device(y, r, z, k)
    after = device(lax.rem(y + r, yn), k, z, 1 - r)
    before = device(lax.rem(y + yn - 1 + r, yn), k, z, 1 - r)
    last_to = device(lax.rem(y + r, yn), 1 - r, z, k)
    last_from = device(lax.rem(y + yn - 1 + k, yn), r, z, 1 - k)
    stays = r == k
    moves = r != k

    part = shard // 2

    def slot_ref(piece, slot):
        if piece == 0:
            return bias.at[slot]
        whole = win if piece < 3 else wout
        first = slot * shard + (piece + 1) % 2 * part
        return whole.at[pl.ds(pl.multiple_of(first, part), part)]

    own = 2 * z + k
    sources = (
        bias_in,
        w_in.at[0, pl.ds(0, part)],
        w_in.at[0, pl.ds(part, part)],
        w_out.at[0, pl.ds(0, part)],
        w_out.at[0, pl.ds(part, part)],
        add_in,
        gain_in,
        shift_in,
        x_in.at[0],
    )

    def own_targets(slot):
        return tuple(slot_ref(piece, slot) for piece in range(PIECES)) + (
            add,
            gain,
            shift,
            x0,
        )

    def own_local(i):
        return pltpu.make_async_copy(sources[i], own_targets(own)[i], own_sem.at[i])

    def own_remote(i, slot):
        return pltpu.make_async_remote_copy(
            src_ref=sources[i],
            dst_ref=own_targets(slot)[i],
            send_sem=own_send.at[i],
            recv_sem=own_sem.at[i],
            device_id=swapped,
            device_id_type=MESH,
        )

    def own_wait(i):
        @pl.when(stays)
        def _():
            own_local(i).wait()

        @pl.when(moves)
        def _():
            own_remote(i, own).wait_recv()

    def patch_load():
        return pltpu.make_async_copy(patches_in, pat, pat_sem.at[0])

    @pl.when(stays)
    def _():
        for i in range(OWN):
            own_local(i).start()

    @pl.when(section == 0)
    def _():
        patch_load().start()

    barrier = pltpu.get_barrier_semaphore()

    def greet(partner):
        pl.semaphore_signal(barrier, inc=1, device_id=partner, device_id_type=MESH)

    for sender in (inward, sibling, before):
        greet(sender)

    @pl.when(moves)
    def _():
        greet(swapped)

    @pl.when((r == 1) & (k == 0))
    def _():
        greet(last_from)

    pl.semaphore_wait(barrier, 3 + r + k - r * k)

    @pl.when(moves)
    def _():
        for i in range(OWN):
            own_remote(i, 2 * z + r).start()

    first_stream = (r, 1 - r)

    def place_at(distance):
        return lax.rem(z + lax.rem(k * 2 * distance + zn - distance, zn), zn)

    def ring(hop, i, piece, arriving):
        ref = slot_ref(piece, 2 * place_at(hop + 1 if arriving else hop) + first_stream[i])
        return pltpu.make_async_remote_copy(
            src_ref=ref,
            dst_ref=ref,
            send_sem=ring_send.at[hop, i, piece],
            recv_sem=ring_recv.at[hop, i, piece],
            device_id=onward,
            device_id_type=MESH,
        )

    def across(distance, i, piece, arriving):
        place = place_at((zn - distance) % zn if arriving else distance)
        ref = slot_ref(piece, 2 * place + first_stream[i])
        return pltpu.make_async_remote_copy(
            src_ref=ref,
            dst_ref=ref,
            send_sem=core_send.at[distance, i, piece],
            recv_sem=core_recv.at[distance, i, piece],
            device_id=sibling,
            device_id_type=MESH,
        )

    for i, mine in ((0, stays), (1, moves)):
        for piece in range(PIECES):

            @pl.when(mine)
            def _():
                own_wait(piece)
                across(0, i, piece, False).start()

            @pl.when(jnp.logical_not(mine))
            def _():
                across(0, i, piece, True).wait_recv()

            ring(0, i, piece, False).start()

    for i in range(PIECES, OWN):
        own_wait(i)
    gain_row = gain[...]
    shift_row = shift[...]
    out_row = add[...]
    normed, widened = normalize(x0[...], gain_row, shift_row)
    normed0[...] = normed
    acc[...] = widened + out_row

    def add_rows(at, bias_here):
        preact = rows_times(normed0[...], win[at, :]) + bias_here
        hidden = activate(preact).astype(jnp.bfloat16)
        acc[...] += jnp.dot(hidden, wout[at, :], preferred_element_type=jnp.float32)

    def add_place(place):
        both = jnp.concatenate(
            [bias[2 * place][0:1, :shard], bias[2 * place + 1][0:1, :shard]], axis=1
        )
        add_rows(pl.ds(pl.multiple_of(place * 2 * shard, 2 * shard), 2 * shard), both)

    def add_stream(place, i):
        slot = 2 * place + first_stream[i]
        add_rows(pl.ds(pl.multiple_of(slot * shard, shard), shard), bias[slot][0:1, :shard])

    def take(hop):
        for i in (0, 1):
            for piece in range(PIECES):
                ring(hop, i, piece, True).wait_recv()
                if hop + 1 < near:
                    ring(hop + 1, i, piece, False).start()
                else:

                    @pl.when(k == 1)
                    def _():
                        ring(hop + 1, i, piece, False).start()

                across(hop + 1, i, piece, False).start()

    def given(distance):
        for i in (0, 1):
            for piece in range(PIECES):
                across(distance, i, piece, True).wait_recv()

    def select_send():
        return pltpu.make_async_remote_copy(
            src_ref=sel,
            dst_ref=sel_far,
            send_sem=sel_send.at[0],
            recv_sem=sel_recv.at[0],
            device_id=swapped,
            device_id_type=MESH,
        )

    add_place(z)
    for hop in range(near):
        take(hop)
        add_place(place_at(hop + 1))
        if hop == 1:

            @pl.when(section == 0)
            def _():
                patch_load().wait()
                for i in range(TICKS - 1):
                    sel[i] = pat[plan[i]]

            @pl.when((section == 0) & (r == 1))
            def _():
                select_send().start()

        if hop >= 2:
            given(hop - 1)
            add_place(place_at(zn - hop + 1))
    for distance in range(max(1, near - 1), near + 1):
        given(distance)
        add_place(place_at(zn - distance))
    for i in (0, 1):

        @pl.when(k == 1)
        def _():
            for piece in range(PIECES):
                ring(near, i, piece, True).wait_recv()
                across(near + 1, i, piece, False).start()

        @pl.when(k == 0)
        def _():
            for piece in range(PIECES):
                across(near + 1, i, piece, True).wait_recv()

        add_stream(place_at(near + 1), i)

    @pl.when((section == 1) & (r == 0))
    def _():
        select_send().wait_recv()

    for first in range(0, 2 * zn, 4):
        bias_row[0:1, pl.ds(first * shard, 4 * shard)] = jnp.concatenate(
            [bias[slot][0:1, :shard] for slot in range(first, first + 4)], axis=1
        )

    def chunk_rows(chunk):
        return pl.ds(chunk * rows, rows)

    def forward(tick, chunk, landing):
        at = chunk_rows(chunk)
        return pltpu.make_async_remote_copy(
            src_ref=prod.at[tick, at],
            dst_ref=landing.at[tick, at],
            send_sem=hop_send.at[tick, chunk],
            recv_sem=hop_recv.at[tick, chunk],
            device_id=after,
            device_id_type=MESH,
        )

    def record(tick, chunk):
        at = chunk_rows(chunk)
        return pltpu.make_async_remote_copy(
            src_ref=prod.at[tick, at],
            dst_ref=result.at[tick, at],
            send_sem=record_send.at[tick, chunk],
            recv_sem=record_recv.at[tick, chunk],
            device_id=last_to,
            device_id_type=MESH,
        )

    result = out.at[0]

    def send_on(tick, chunk):
        @pl.when(moves)
        def _():
            forward(tick, chunk, result).start()

        @pl.when(stays)
        def _():
            @pl.when(tick < TICKS - 1)
            def _():
                forward(tick, chunk, arr).start()

            record(tick, chunk).start()

    for chunk in range(CHUNKS):
        prod[0, chunk_rows(chunk)] = acc[chunk_rows(chunk), :].astype(jnp.bfloat16)
        send_on(0, chunk)

    wide = 256

    def step(tick, chunk):
        at = chunk_rows(chunk)

        @pl.when(stays)
        def _():
            forward(tick - 1, chunk, result).wait_recv()
            cur[...] = out[0, tick - 1, at, :]

        @pl.when(moves)
        def _():
            forward(tick - 1, chunk, arr).wait_recv()
            cur[...] = arr[tick - 1, at, :]

        @pl.when((section == 0) & (r == 0))
        def _():
            cur[...] = sel[tick - 1, at, :]

        @pl.when((section == 1) & (r == 0))
        def _():
            cur[...] = sel_far[tick - 1, at, :]

        normed, widened = normalize(cur[...], gain_row, shift_row)
        for low in range(0, width, wide):
            preact = rows_times(normed, win[low : low + wide, :]) + bias_row[0:1, low : low + wide]
            hid[:, low : low + wide] = activate(preact).astype(jnp.bfloat16)
        for low in range(0, depth, wide):
            mixed = jnp.dot(
                hid[...], wout[:, low : low + wide], preferred_element_type=jnp.float32
            )
            prod[tick, at, low : low + wide] = (
                widened[:, low : low + wide] + mixed + out_row[:, low : low + wide]
            ).astype(jnp.bfloat16)

        send_on(tick, chunk)

    @pl.loop(1, TICKS)
    def _(tick):
        for chunk in range(CHUNKS):
            step(tick, chunk)

    @pl.when(moves)
    def _():
        for tick in range(TICKS):
            for chunk in range(CHUNKS):
                record(tick, chunk).wait_recv()
                forward(tick, chunk, result).wait_send()

    @pl.when(stays)
    def _():
        for tick in range(TICKS):
            for chunk in range(CHUNKS):
                if tick == TICKS - 1:
                    forward(tick, chunk, result).wait_recv()
                else:
                    forward(tick, chunk, arr).wait_send()
                record(tick, chunk).wait_send()

    @pl.when(moves)
    def _():
        for i in range(OWN):
            own_remote(i, 2 * z + r).wait_send()

    @pl.when((section == 0) & (r == 1))
    def _():
        select_send().wait_send()

    for i, mine in ((0, stays), (1, moves)):
        for piece in range(PIECES):

            @pl.when(mine)
            def _():
                across(0, i, piece, False).wait_send()

            for hop in range(near):
                ring(hop, i, piece, False).wait_send()
                across(hop + 1, i, piece, False).wait_send()

            @pl.when(k == 1)
            def _():
                ring(near, i, piece, False).wait_send()
                across(near + 1, i, piece, False).wait_send()


def shards(
    section_inputs, w_in, in_bias, w_out, out_bias, norm_gain, norm_bias, patches, plan, *, yn, zn
):
    tokens, depth = section_inputs.shape[1:]
    shard = w_in.shape[1]
    width = 2 * zn * shard
    bias_tile = jnp.pad(in_bias.astype(jnp.float32), ((0, 7), (0, -shard % 128)))
    anywhere = pl.BlockSpec(memory_space=pl.ANY)
    half = zn // 2
    dma = pltpu.SemaphoreType.DMA
    return pl.pallas_call(
        functools.partial(block_kernel, yn, zn),
        out_shape=pltpu.VMEM((1, TICKS, tokens, depth), jnp.bfloat16),
        in_specs=[anywhere] * 8 + [pl.BlockSpec(memory_space=pltpu.SMEM)],
        out_specs=pl.BlockSpec(memory_space=pltpu.VMEM),
        scratch_shapes=[
            pltpu.VMEM((tokens, depth), jnp.bfloat16),
            pltpu.VMEM((width, depth), jnp.bfloat16),
            pltpu.VMEM((width, depth), jnp.bfloat16),
            pltpu.VMEM((1, depth), jnp.float32),
            pltpu.VMEM((1, depth), jnp.float32),
            pltpu.VMEM((1, depth), jnp.float32),
            pltpu.VMEM((2 * zn, 8, 128), jnp.float32),
            pltpu.VMEM((8, width), jnp.float32),
            pltpu.VMEM(patches.shape, jnp.bfloat16),
            pltpu.VMEM((TICKS - 1, tokens, depth), jnp.bfloat16),
            pltpu.VMEM((TICKS - 1, tokens, depth), jnp.bfloat16),
            pltpu.VMEM((tokens // CHUNKS, depth), jnp.bfloat16),
            pltpu.VMEM((tokens, depth), jnp.bfloat16),
            pltpu.VMEM((tokens, depth), jnp.float32),
            pltpu.VMEM((tokens // CHUNKS, width), jnp.bfloat16),
            pltpu.VMEM((TICKS, tokens, depth), jnp.bfloat16),
            pltpu.VMEM((TICKS - 1, tokens, depth), jnp.bfloat16),
            dma((OWN,)),
            dma((OWN,)),
            dma((half, 2, PIECES)),
            dma((half, 2, PIECES)),
            dma((half + 1, 2, PIECES)),
            dma((half + 1, 2, PIECES)),
            dma((1,)),
            dma((1,)),
            dma((1,)),
            dma((TICKS, CHUNKS)),
            dma((TICKS, CHUNKS)),
            dma((TICKS, CHUNKS)),
            dma((TICKS, CHUNKS)),
        ],
        compiler_params=pltpu.CompilerParams(collective_id=0, has_side_effects=True),
    )(section_inputs, w_in, w_out, bias_tile, out_bias, norm_gain, norm_bias, patches, plan)


def solution(mesh):
    placed = (
        P("section", "tensor", None),
        P("section", "tensor", None),
        P("section", "tensor"),
        P("section", "tensor", None),
        P("section", None),
        P("section", None),
        P("section", None),
        P(None, "tensor", None),
        P(),
    )
    return jax.shard_map(
        functools.partial(
            shards, yn=mesh.shape["section"] // 2, zn=mesh.shape["tensor"] // 2
        ),
        mesh=mesh,
        in_specs=placed,
        out_specs=P("section", None, "tensor", None),
        check_vma=False,
    )
```

time: 109 us -> 106 us (0.972)
  Pallas kernels: 104 us -> 102 us
  local copies, waits for them, and re-layouts: 2.26 us -> 0.97 us
    pallas_call x1, Pallas kernels: 104 us -> 102 us  [shards(): pl.pallas_call(functools.partial(block_kernel, yn, zn), out_shape=pltpu.V...]
    concatenate x2 -> x0, other arithmetic: 1.36 us -> none  [the longest x1 0.74 us: shards(): jnp.concatenate([out_bias, norm_gain, norm_bias])]
    unnamed x1, local copies, waits for them, and re-layouts: 2.26 us -> 0.97 us
where the time goes in v3:
time: 106 us; the launch traced here: 105 us
  Pallas kernels  102 us (96%)
  other arithmetic  1.25 us (1%)
    pallas_call x1, Pallas kernels, shards(): pl.pallas_call(functools.partial(block_kernel, yn, zn), out_shape=pltpu.V...  102 us

profile of v3, /device:TPU:1, one launch (start us, length us, event | category | flops | bytes accessed | tf_op | source)
XLA Modules:
  0.0 104.6 jit_solution(7765127658753611514)
XLA Ops:
  0.0 1.3 %pad_convert_fusion.bias_in = f32[8,128]{1,0:T(8,128)} fusion(bf16[1,96]{1,0:T(2,128)(2,1)} %param.11), kind=kLoop, calls=%fused_computation | loop fusion | flops 1024 | bytes 4288 | tf_op jit(solution)/shard_map/jit(_pad)/pad | solution.py:438
  1.3 102.4 %shard_map.91 = bf16[1,4,128,1024]{3,2,1,0:T(8,128)(2,1)S(1)} custom-call(bf16[1,128,1024]{2,1,0:T(8,128)(2,1)} %x_in.1, bf16[1,96,1024]{2,1,0:T(8,128)(2,1)} %w_in.1, bf16[1,96,1024]{2,1,0:T(8,128)(2,1)} %w_out.1, f32[8,128]{1,0:T(8,128)} %pad_convert_fusion.bias_in, f32[1,1024]{1,0:T(1,128)} %add_in.1, f32[1,1024]{1,0:T(1,128)} %gain_in.1, ...), custom_call_target="tpu_custom_call" | custom-call | tf_op jit(solution)/shard_map/pallas_call | solution.py:442
  103.7 1.0 copy.11

commit v4 on v3

--- a/solution.py
+++ b/solution.py
@@ -14,8 +14,8 @@
 norm_floor = 0.1
 gelu_slope = 1.702
 
-OWN = 9
-PIECES = 5
+OWN = 7
+PIECES = 3
 
 
 def normalize(current, gain_row, shift_row):
@@ -72,22 +72,17 @@
     stays = r == k
     moves = r != k
 
-    part = shard // 2
-
     def slot_ref(piece, slot):
         if piece == 0:
             return bias.at[slot]
-        whole = win if piece < 3 else wout
-        first = slot * shard + (piece + 1) % 2 * part
-        return whole.at[pl.ds(pl.multiple_of(first, part), part)]
+        whole = win if piece == 1 else wout
+        return whole.at[pl.ds(pl.multiple_of(slot * shard, shard), shard)]
 
     own = 2 * z + k
     sources = (
         bias_in,
-        w_in.at[0, pl.ds(0, part)],
-        w_in.at[0, pl.ds(part, part)],
-        w_out.at[0, pl.ds(0, part)],
-        w_out.at[0, pl.ds(part, part)],
+        w_in.at[0],
+        w_out.at[0],
         add_in,
         gain_in,
         shift_in,
@@ -210,6 +205,9 @@
     normed0[...] = normed
     acc[...] = widened + out_row
 
+    def bias_of(slot):
+        return bias[slot].astype(jnp.float32)
+
     def add_rows(at, bias_here):
         preact = rows_times(normed0[...], win[at, :]) + bias_here
         hidden = activate(preact).astype(jnp.bfloat16)
@@ -217,13 +215,13 @@
 
     def add_place(place):
         both = jnp.concatenate(
-            [bias[2 * place][0:1, :shard], bias[2 * place + 1][0:1, :shard]], axis=1
+            [bias_of(2 * place), bias_of(2 * place + 1)], axis=1
         )
         add_rows(pl.ds(pl.multiple_of(place * 2 * shard, 2 * shard), 2 * shard), both)
 
     def add_stream(place, i):
         slot = 2 * place + first_stream[i]
-        add_rows(pl.ds(pl.multiple_of(slot * shard, shard), shard), bias[slot][0:1, :shard])
+        add_rows(pl.ds(pl.multiple_of(slot * shard, shard), shard), bias_of(slot))
 
     def take(hop):
         for i in (0, 1):
@@ -297,7 +295,7 @@
 
     for first in range(0, 2 * zn, 4):
         bias_row[0:1, pl.ds(first * shard, 4 * shard)] = jnp.concatenate(
-            [bias[slot][0:1, :shard] for slot in range(first, first + 4)], axis=1
+            [bias_of(slot) for slot in range(first, first + 4)], axis=1
         )
 
     def chunk_rows(chunk):
@@ -435,7 +433,6 @@
     tokens, depth = section_inputs.shape[1:]
     shard = w_in.shape[1]
     width = 2 * zn * shard
-    bias_tile = jnp.pad(in_bias.astype(jnp.float32), ((0, 7), (0, -shard % 128)))
     anywhere = pl.BlockSpec(memory_space=pl.ANY)
     half = zn // 2
     dma = pltpu.SemaphoreType.DMA
@@ -451,7 +448,7 @@
             pltpu.VMEM((1, depth), jnp.float32),
             pltpu.VMEM((1, depth), jnp.float32),
             pltpu.VMEM((1, depth), jnp.float32),
-            pltpu.VMEM((2 * zn, 8, 128), jnp.float32),
+            pltpu.VMEM((2 * zn, 1, shard), jnp.bfloat16),
             pltpu.VMEM((8, width), jnp.float32),
             pltpu.VMEM(patches.shape, jnp.bfloat16),
             pltpu.VMEM((TICKS - 1, tokens, depth), jnp.bfloat16),
@@ -477,7 +474,7 @@
             dma((TICKS, CHUNKS)),
         ],
         compiler_params=pltpu.CompilerParams(collective_id=0, has_side_effects=True),
-    )(section_inputs, w_in, w_out, bias_tile, out_bias, norm_gain, norm_bias, patches, plan)
+    )(section_inputs, w_in, w_out, in_bias, out_bias, norm_gain, norm_bias, patches, plan)
 
 
 def solution(mesh):

time: 106 us -> 103 us (0.972)
  other arithmetic: 1.25 us -> 0 us
    pallas_call x1, Pallas kernels: 102 us -> 101 us  [shards(): pl.pallas_call(functools.partial(block_kernel, yn, zn), out_shape=pltpu.V...]
    pad x1 -> x0, other arithmetic: 1.25 us -> none  [shards(): jnp.pad(in_bias.astype(jnp.float32), ((0, 7), (0, -shard % 128)))]
where the time goes in v4:
time: 103 us; the launch traced here: 102 us
  Pallas kernels  101 us (98%)
    pallas_call x1, Pallas kernels, shards(): pl.pallas_call(functools.partial(block_kernel, yn, zn), out_shape=pltpu.V...  101 us

profile of v4, /device:TPU:1, one launch (start us, length us, event | category | flops | bytes accessed | tf_op | source)
XLA Modules:
  0.0 102.1 jit_solution(9619425610353414051)
XLA Ops:
  0.0 101.1 %shard_map.91 = bf16[1,4,128,1024]{3,2,1,0:T(8,128)(2,1)S(1)} custom-call(bf16[1,128,1024]{2,1,0:T(8,128)(2,1)} %x_in.1, bf16[1,96,1024]{2,1,0:T(8,128)(2,1)} %w_in.1, bf16[1,96,1024]{2,1,0:T(8,128)(2,1)} %w_out.1, bf16[1,96]{1,0:T(2,128)(2,1)} %bias_in.1, f32[1,1024]{1,0:T(1,128)} %add_in.1, f32[1,1024]{1,0:T(1,128)} %gain_in.1, f32[1,1024]{1,0:T(1,128)} %shift_in.1, ...), custom_call_target="tpu_custom_call" | custom-call | tf_op jit(solution)/shard_map/pallas_call | solution.py:439
  101.1 1.0 copy.11

commit v5 on v4

--- a/solution.py
+++ b/solution.py
@@ -323,6 +323,17 @@
             device_id_type=MESH,
         )
 
+    def hand_back(tick, chunk):
+        at = chunk_rows(chunk)
+        return pltpu.make_async_remote_copy(
+            src_ref=arr.at[tick, at],
+            dst_ref=result.at[tick, at],
+            send_sem=record_send.at[tick, chunk],
+            recv_sem=record_recv.at[tick, chunk],
+            device_id=swapped,
+            device_id_type=MESH,
+        )
+
     result = out.at[0]
 
     def send_on(tick, chunk):
@@ -336,7 +347,9 @@
             def _():
                 forward(tick, chunk, arr).start()
 
-            record(tick, chunk).start()
+            @pl.when((tick == TICKS - 1) | (r == 0))
+            def _():
+                record(tick, chunk).start()
 
     for chunk in range(CHUNKS):
         prod[0, chunk_rows(chunk)] = acc[chunk_rows(chunk), :].astype(jnp.bfloat16)
@@ -356,6 +369,10 @@
         def _():
             forward(tick - 1, chunk, arr).wait_recv()
             cur[...] = arr[tick - 1, at, :]
+
+            @pl.when(r == 0)
+            def _():
+                hand_back(tick - 1, chunk).start()
 
         @pl.when((section == 0) & (r == 0))
         def _():
@@ -390,6 +407,11 @@
             for chunk in range(CHUNKS):
                 record(tick, chunk).wait_recv()
                 forward(tick, chunk, result).wait_send()
+                if tick < TICKS - 1:
+
+                    @pl.when(r == 0)
+                    def _():
+                        hand_back(tick, chunk).wait_send()
 
     @pl.when(stays)
     def _():
@@ -397,9 +419,13 @@
             for chunk in range(CHUNKS):
                 if tick == TICKS - 1:
                     forward(tick, chunk, result).wait_recv()
+                    record(tick, chunk).wait_send()
                 else:
                     forward(tick, chunk, arr).wait_send()
-                record(tick, chunk).wait_send()
+
+                    @pl.when(r == 0)
+                    def _():
+                        record(tick, chunk).wait_send()
 
     @pl.when(moves)
     def _():

time: 103 us -> 101 us (0.981); the launches traced: 102 us -> 101 us
  no operation moved by 1% of the time
where the time goes in v5:
time: 101 us
  Pallas kernels  100 us (99%)
    pallas_call x1, Pallas kernels, shards(): pl.pallas_call(functools.partial(block_kernel, yn, zn), out_shape=pltpu.V...  100 us

profile of v5, /device:TPU:1, one launch (start us, length us, event | category | flops | bytes accessed | tf_op | source)
XLA Modules:
  0.0 101.2 jit_solution(2732340263271470650)
XLA Ops:
  0.0 100.2 %shard_map.91 = bf16[1,4,128,1024]{3,2,1,0:T(8,128)(2,1)S(1)} custom-call(bf16[1,128,1024]{2,1,0:T(8,128)(2,1)} %x_in.1, bf16[1,96,1024]{2,1,0:T(8,128)(2,1)} %w_in.1, bf16[1,96,1024]{2,1,0:T(8,128)(2,1)} %w_out.1, bf16[1,96]{1,0:T(2,128)(2,1)} %bias_in.1, f32[1,1024]{1,0:T(1,128)} %add_in.1, f32[1,1024]{1,0:T(1,128)} %gain_in.1, f32[1,1024]{1,0:T(1,128)} %shift_in.1, ...), custom_call_target="tpu_custom_call" | custom-call | tf_op jit(solution)/shard_map/pallas_call | solution.py:465
  100.2 1.0 copy.11

commit v6 on v5

--- a/solution.py
+++ b/solution.py
@@ -347,7 +347,7 @@
             def _():
                 forward(tick, chunk, arr).start()
 
-            @pl.when((tick == TICKS - 1) | (r == 0))
+            @pl.when((tick == TICKS - 1) | (tick == 1) | (r == 0))
             def _():
                 record(tick, chunk).start()
 
@@ -370,7 +370,7 @@
             forward(tick - 1, chunk, arr).wait_recv()
             cur[...] = arr[tick - 1, at, :]
 
-            @pl.when(r == 0)
+            @pl.when((r == 0) & (tick != 2))
             def _():
                 hand_back(tick - 1, chunk).start()
 
@@ -407,7 +407,7 @@
             for chunk in range(CHUNKS):
                 record(tick, chunk).wait_recv()
                 forward(tick, chunk, result).wait_send()
-                if tick < TICKS - 1:
+                if tick < TICKS - 1 and tick != 1:
 
                     @pl.when(r == 0)
                     def _():
@@ -423,7 +423,7 @@
                 else:
                     forward(tick, chunk, arr).wait_send()
 
-                    @pl.when(r == 0)
+                    @pl.when((r == 0) | (tick == 1))
                     def _():
                         record(tick, chunk).wait_send()
 

time: 101 us -> 102 us (level); the launches traced: 101 us -> 99.9 us
  Pallas kernels: 100 us -> 98.9 us
    pallas_call x1, Pallas kernels: 100 us -> 98.9 us  [shards(): pl.pallas_call(functools.partial(block_kernel, yn, zn), out_shape=pltpu.V...]
where the time goes in v6:
time: 102 us; the launch traced here: 99.9 us
  Pallas kernels  98.9 us (97%)
    pallas_call x1, Pallas kernels, shards(): pl.pallas_call(functools.partial(block_kernel, yn, zn), out_shape=pltpu.V...  98.9 us

profile of v6, /device:TPU:1, one launch (start us, length us, event | category | flops | bytes accessed | tf_op | source)
XLA Modules:
  0.0 99.9 jit_solution(6795167357634347523)
XLA Ops:
  0.0 98.9 %shard_map.91 = bf16[1,4,128,1024]{3,2,1,0:T(8,128)(2,1)S(1)} custom-call(bf16[1,128,1024]{2,1,0:T(8,128)(2,1)} %x_in.1, bf16[1,96,1024]{2,1,0:T(8,128)(2,1)} %w_in.1, bf16[1,96,1024]{2,1,0:T(8,128)(2,1)} %w_out.1, bf16[1,96]{1,0:T(2,128)(2,1)} %bias_in.1, f32[1,1024]{1,0:T(1,128)} %add_in.1, f32[1,1024]{1,0:T(1,128)} %gain_in.1, f32[1,1024]{1,0:T(1,128)} %shift_in.1, ...), custom_call_target="tpu_custom_call" | custom-call | tf_op jit(solution)/shard_map/pallas_call | solution.py:465
  98.9 1.0 copy.11
